TPU v7x, 32 devices: a whole 2x2x4 slice. The times are simulated.
32 devices in a mesh: group: 4 (over y, core), local: 8 (over z, x).
Axes of the slice: x: 2, y: 2, z: 4, core: 2. Of those that a mesh axis runs over, the one named last changes fastest.
Arguments:
- lookup_grads: bfloat16 [262144, 256], P(('group', 'local')), may hold values from -0.29882812 to 0.29882812
- slot_index: int32 [2, 262144], P(None, ('group', 'local')), may hold values from 0 to 511, as said below
- unique_rows: int32 [2, 2048], P(None, ('group', 'local')), may hold values from -1 to 32767, as said below
- tables: float32 [2, 32768, 256], P(None, ('group', 'local')), may hold values from -6 to 6
- accums: float32 [2, 32768], P(None, ('group', 'local')), may hold values from 0.01 to 1
Outputs:
- new_tables: float32 [2, 32768, 256], P(None, ('group', 'local'))
- new_accums: float32 [2, 32768], P(None, ('group', 'local'))
Inputs may be any that keep to these rules, and one draw needn't show every extreme that they name: slot_index[t, i] names a slot of lookup i's group list whose entry in unique_rows[t] is not -1. `unique_rows`: table row p is owned by device p // 1024, which is device (group p // 8192, local p // 1024 % 8). Group g's list is entries g * 512 to (g + 1) * 512 - 1; its block l of 64 entries consists of 4 buckets of 16 entries, bucket h holding only rows owned by device (group h, local l), the used entries first and -1 after them. Rows within a group's list are distinct. In every draw and table some device (group h, local l) gets a full bucket from every group.
All inputs are finite; a program needn't handle non-finite values.
Results may differ from a plain program's by a relative error of at most 0.0003.
Values sent between devices are 32-bit elements; how exact they have to be, the bound alone decides.
A program may use at most 64 MiB of HBM per device.

v0:
```python
import functools

import jax
import jax.numpy as jnp
from jax import lax
from jax.experimental import pallas as pl
from jax.experimental.pallas import tpu as pltpu
from jax.sharding import PartitionSpec as P

learning_rate = 0.1
epsilon = 1e-08
MESH = pl.DeviceIdType.MESH
PIECES = 2
BLOCKS = 4


def exchange_kernel(
    n_group, n_local, chunk, grads_hbm, index_hbm, rows_hbm, packed_ref,
    grads, index, rows, sums, pair, recv, rows_recv, acc,
    grad_sems, index_sem, rows_sem, pair_sems, pair_send_sem, send_sem, recv_sem, row_send_sem, row_recv_sem,
):
    group, local = lax.axis_index("group"), lax.axis_index("local")
    n_dev = n_group * n_local
    me = group * n_local + local
    look, width = grads.shape
    capacity = sums.shape[2]
    n_chunk = look // chunk
    peers = n_local // BLOCKS
    buckets = peers * n_group
    rows_block = buckets * capacity
    block_me, peer_me = local // peers, lax.rem(local, peers)

    index_load = pltpu.make_async_copy(index_hbm, index, index_sem)
    rows_load = pltpu.make_async_copy(rows_hbm, rows, rows_sem)

    def load(k):
        at = pl.ds(k * chunk, chunk)
        return pltpu.make_async_copy(grads_hbm.at[at], grads.at[at], grad_sems.at[k])

    index_load.start()
    for k in range(n_chunk):
        load(k).start()
    rows_load.start()

    barrier = pltpu.get_barrier_semaphore()

    def greet(o, c):
        to = lax.rem(me + o, n_dev)
        pl.semaphore_signal(
            barrier, inc=1, device_id={"group": to // n_local, "local": lax.rem(to, n_local)},
            device_id_type=MESH,
        )
        return c

    lax.fori_loop(1, n_dev, greet, 0)

    def send_pair(block, o, h):
        to = block * peers + lax.rem(peer_me + o, peers)
        return pltpu.make_async_remote_copy(
            src_ref=sums.at[to * n_group + h],
            dst_ref=pair.at[(block * n_group + h) * (peers - 1) + (peers - 1 - o)],
            send_sem=pair_send_sem, recv_sem=pair_sems.at[block * n_group + h],
            device_id={"group": group, "local": block_me * peers + lax.rem(peer_me + o, peers)},
            device_id_type=MESH,
        )

    def send_bucket(l, h, place):
        return pltpu.make_async_remote_copy(
            src_ref=sums.at[l * n_group + h], dst_ref=recv.at[group * places + place],
            send_sem=send_sem, recv_sem=recv_sem,
            device_id={"group": h, "local": l}, device_id_type=MESH,
        )

    def send_rows(h):
        return pltpu.make_async_remote_copy(
            src_ref=rows, dst_ref=rows_recv.at[group],
            send_sem=row_send_sem, recv_sem=row_recv_sem,
            device_id={"group": h, "local": local}, device_id_type=MESH,
        )

    places = BLOCKS - 1 + peers
    order = (2, 1, 3, 0)

    def block_at(step):
        return lax.rem(block_me + order[step], BLOCKS)

    def sum_block(step):
        block = block_at(step)
        targets = lax.broadcasted_iota(jnp.int32, (rows_block, chunk), 0) + block * rows_block

        def body(k, c):
            if step == 0:
                load(k).wait()
            at = pl.ds(pl.multiple_of(k * chunk, chunk), chunk)
            onehot = jnp.concatenate(
                [jnp.where(index[t : t + 1, at] == targets, 1.0, 0.0).astype(jnp.bfloat16) for t in range(2)],
                axis=0,
            )
            acc[...] += jnp.dot(onehot, grads[at, :], preferred_element_type=jnp.float32)
            return c

        acc[...] = jnp.zeros_like(acc)
        if step == 0:
            index_load.wait()
        lax.fori_loop(0, n_chunk, body, 0)
        for t in range(2):
            sums[pl.ds(block * buckets, buckets), t] = acc[t * rows_block : (t + 1) * rows_block, :].reshape(
                buckets, capacity, width
            )

    def start_pairs(step):
        def one(i, c):
            send_pair(block_at(step), 1 + i // n_group, lax.rem(group + lax.rem(i, n_group), n_group)).start()
            return c

        lax.fori_loop(0, (peers - 1) * n_group, one, 0)

    def pass_on(step, start, stop):
        block = block_at(step)
        mine = block * peers + peer_me

        def one(i, c):
            h = lax.rem(group + i, n_group)
            first = (block * n_group + h) * (peers - 1)
            pltpu.make_async_remote_copy(
                src_ref=pair.at[pl.ds(first, peers - 1)], dst_ref=pair.at[pl.ds(first, peers - 1)],
                send_sem=pair_send_sem, recv_sem=pair_sems.at[block * n_group + h],
                device_id={"group": group, "local": local}, device_id_type=MESH,
            ).wait_recv()
            total = sums[mine * n_group + h]
            for p in range(peers - 1):
                total = total + pair[first + p]
            sums[mine * n_group + h] = total
            send_bucket(mine, h, order[step] - 1).start()
            return c

        lax.fori_loop(start, stop, one, 0)

    sum_block(0)
    pl.semaphore_wait(barrier, n_dev - 1)
    start_pairs(0)
    rows_load.wait()

    def row_step(o, c):
        send_rows(lax.rem(group + o, n_group)).start()
        return c

    lax.fori_loop(1, n_group, row_step, 0)
    for step in range(1, BLOCKS - 1):
        sum_block(step)
        start_pairs(step)
        if step == 1:
            pass_on(0, 0, n_group // 2)
    pass_on(0, n_group // 2, n_group)
    sum_block(BLOCKS - 1)

    def own_step(i, c):
        l = block_me * peers + lax.rem(peer_me + i // n_group, peers)
        send_bucket(l, lax.rem(group + i, n_group), BLOCKS - 1 + peer_me).start()
        return c

    lax.fori_loop(1, buckets, own_step, 0)
    for step in range(1, BLOCKS - 1):
        pass_on(step, 0, n_group)

    recv[group * places + BLOCKS - 1 + peer_me] = sums[local * n_group + group]
    rows_recv[group] = rows[...]
    parts = n_group * places - 1
    everyone = pltpu.make_async_remote_copy(
        src_ref=recv.at[pl.ds(0, parts)], dst_ref=recv.at[pl.ds(0, parts)],
        send_sem=send_sem, recv_sem=recv_sem,
        device_id={"group": group, "local": local}, device_id_type=MESH,
    )
    row_wait = pltpu.make_async_remote_copy(
        src_ref=rows_recv.at[pl.ds(0, n_group - 1)], dst_ref=rows_recv.at[pl.ds(0, n_group - 1)],
        send_sem=row_send_sem, recv_sem=row_recv_sem,
        device_id={"group": group, "local": local}, device_id_type=MESH,
    )
    row_wait.wait_recv()
    slots = rows.shape[1]
    packed_ref[2 * slots :, :] = jnp.zeros_like(packed_ref[2 * slots :, :])
    for g in range(n_group):
        at = 2 * slots + 2 * g
        packed_ref[at : at + 2, 0:slots] = rows_recv[g].astype(jnp.float32)
    row_wait.wait_send()
    pair_wait_parts = (BLOCKS - 1) * n_group * (peers - 1)
    pltpu.make_async_remote_copy(
        src_ref=pair.at[pl.ds(0, pair_wait_parts)], dst_ref=pair.at[pl.ds(0, pair_wait_parts)],
        send_sem=pair_send_sem, recv_sem=recv_sem,
        device_id={"group": group, "local": local}, device_id_type=MESH,
    ).wait_send()
    everyone.wait_send()
    everyone.wait_recv()
    for g in range(n_group):
        for t in range(2):
            total = recv[g * places, t]
            for p in range(1, places):
                total = total + recv[g * places + p, t]
            at = t * slots + g * capacity
            packed_ref[at : at + capacity, :] = total


def update_kernel(n_group, slots, packed_ref, tables_ref, accums_ref, new_tables_hbm, new_accums_ref, new, out_sems):
    group, local = lax.axis_index("group"), lax.axis_index("local")
    n_local = lax.axis_size("local")
    rows_dev, width = tables_ref.shape[1:]
    capacity = slots // n_group
    base = ((group * n_local + local) * rows_dev).astype(jnp.float32)
    slot_at = lax.broadcasted_iota(jnp.int32, (capacity, slots), 0)
    lane_at = lax.broadcasted_iota(jnp.int32, (capacity, slots), 1)
    first_at = lax.broadcasted_iota(jnp.int32, (slots, slots), 0)
    second_at = lax.broadcasted_iota(jnp.int32, (slots, slots), 1)
    row_lane = lax.broadcasted_iota(jnp.int32, (slots, rows_dev), 1).astype(jnp.float32)
    piece = rows_dev // PIECES
    piece_row = lax.broadcasted_iota(jnp.int32, (piece, 3 * slots), 0).astype(jnp.float32)

    def out(t, i):
        at = pl.ds(i * piece, piece)
        return pltpu.make_async_copy(new.at[t, at], new_tables_hbm.at[t, at], out_sems.at[t, i])

    for t in range(2):
        columns = []
        for g in range(n_group):
            mine = lane_at == slot_at + group * capacity
            at = 2 * slots + 2 * g + t
            columns.append(jnp.sum(jnp.where(mine, packed_ref[at : at + 1, 0:slots], 0.0), axis=1, keepdims=True))
        column = jnp.concatenate(columns, axis=0)
        column = jnp.where(column < 0.0, -1.0, column - base)
        as_row = jnp.sum(jnp.where(first_at == second_at, column, 0.0), axis=0, keepdims=True)
        same = column == as_row
        totals = jnp.dot(
            jnp.where(same, 1.0, 0.0), packed_ref[t * slots : (t + 1) * slots, :],
            preferred_element_type=jnp.float32, precision=lax.Precision.HIGHEST,
        )
        squares = jnp.mean(totals * totals, axis=1, keepdims=True)
        hit = row_lane == column
        accums = accums_ref[t : t + 1, :]
        old = jnp.sum(jnp.where(hit, accums, 0.0), axis=1, keepdims=True)
        added = jnp.max(jnp.where(hit, squares, 0.0), axis=0, keepdims=True)
        new_accums_ref[t : t + 1, :] = accums + added
        change = learning_rate * totals / (jnp.sqrt(old + squares) + epsilon)
        earlier = jnp.max(jnp.where(same & (first_at < second_at), 1.0, 0.0), axis=0, keepdims=True)
        target = jnp.where(earlier > 0.0, -1.0, as_row)
        target = jnp.concatenate([target] * 3, axis=1)
        high = change.astype(jnp.bfloat16)
        rest = change - high.astype(jnp.float32)
        middle = rest.astype(jnp.bfloat16)
        low = (rest - middle.astype(jnp.float32)).astype(jnp.bfloat16)
        parts = jnp.concatenate([high, middle, low], axis=0)
        for i in range(PIECES):
            at = slice(i * piece, (i + 1) * piece)
            onehot = jnp.where(piece_row + float(i * piece) == target, 1.0, 0.0).astype(jnp.bfloat16)
            new[t, at] = tables_ref[t, at] - jnp.dot(onehot, parts, preferred_element_type=jnp.float32)
            out(t, i).start()
    for t in range(2):
        for i in range(PIECES):
            out(t, i).wait()


def local_step(n_group, n_local, lookup_grads, slot_index, unique_rows, tables, accums):
    look, width = lookup_grads.shape
    slots = unique_rows.shape[1]
    capacity = slots // n_group
    n_dev = n_group * n_local
    rows_dev = tables.shape[1]
    chunk = min(4096, look)
    peers = n_local // BLOCKS
    block_rows = 2 * (slots * n_local // BLOCKS)
    vmem = pl.BlockSpec(memory_space=pltpu.VMEM)
    hbm = pl.BlockSpec(memory_space=pltpu.HBM)
    dma = pltpu.SemaphoreType.DMA
    packed = pl.pallas_call(
        functools.partial(exchange_kernel, n_group, n_local, chunk),
        out_shape=jax.ShapeDtypeStruct((2 * slots + -(-2 * n_group // 8) * 8, width), jnp.float32),
        in_specs=[hbm, hbm, hbm],
        out_specs=vmem,
        scratch_shapes=[
            pltpu.VMEM((look, width), jnp.bfloat16),
            pltpu.VMEM((2, look), jnp.int32),
            pltpu.VMEM((2, slots), jnp.int32),
            pltpu.VMEM((n_dev, 2, capacity, width), jnp.float32),
            pltpu.VMEM((BLOCKS * n_group * (peers - 1), 2, capacity, width), jnp.float32),
            pltpu.VMEM((n_group * (BLOCKS - 1 + peers), 2, capacity, width), jnp.float32),
            pltpu.VMEM((n_group, 2, slots), jnp.int32),
            pltpu.VMEM((block_rows, width), jnp.float32),
            dma((look // chunk,)), dma, dma, dma((BLOCKS * n_group,)), dma, dma, dma, dma, dma,
        ],
        compiler_params=pltpu.CompilerParams(
            collective_id=0, has_side_effects=True, vmem_limit_bytes=63 * 10**6
        ),
        cost_estimate=pl.CostEstimate(flops=2 * 2 * look * width * slots * n_local, bytes_accessed=2 * look * width, transcendentals=0),
    )(lookup_grads, slot_index, unique_rows)
    return pl.pallas_call(
        functools.partial(update_kernel, n_group, slots),
        out_shape=(
            jax.ShapeDtypeStruct(tables.shape, jnp.float32),
            jax.ShapeDtypeStruct(accums.shape, jnp.float32),
        ),
        in_specs=[vmem, vmem, vmem],
        out_specs=(hbm, vmem),
        scratch_shapes=[
            pltpu.VMEM((2, rows_dev, width), jnp.float32),
            dma((2, PIECES)),
        ],
        compiler_params=pltpu.CompilerParams(vmem_limit_bytes=24 * 2**20),
    )(packed, tables, accums)


def solution(mesh):
    n_group, n_local = mesh.shape["group"], mesh.shape["local"]
    return jax.shard_map(
        functools.partial(local_step, n_group, n_local),
        mesh=mesh,
        in_specs=(
            P(("group", "local"), None),
            P(None, ("group", "local")),
            P(None, ("group", "local")),
            P(None, ("group", "local"), None),
            P(None, ("group", "local")),
        ),
        out_specs=(P(None, ("group", "local"), None), P(None, ("group", "local"))),
        check_vma=False,
    )
```

profile of v0, /device:TPU:0, one launch (start us, length us, event | category | flops | bytes accessed | tf_op | source)
XLA Modules:
  0.0 27.6 jit_solution(16879605417167782270)
XLA Ops:
  0.6 0.0 copy-start.2
  0.6 0.0 copy-start
  0.7 23.0 %shard_map.68.packed_ref = f32[136,256]{1,0:T(8,128)} custom-call(bf16[8192,256]{1,0:T(8,128)(2,1)} %grads_hbm.1, s32[2,8192]{1,0:T(2,128)} %index_hbm.1, s32[2,64]{1,0:T(2,128)} %rows_hbm.1), custom_call_target="tpu_custom_call" | custom-call | flops 4294967296 | bytes 4194304 | tf_op jit(solution)/shard_map/pallas_call | solution.py:272
  23.7 0.0 copy-done.2
  23.7 0.0 copy-done
  23.7 0.0 copy-start.1
  23.7 0.9 %copy-done.1 = f32[136,256]{1,0:T(8,128)S(1)} copy-done((f32[136,256]{1,0:T(8,128)S(1)}, f32[136,256]{1,0:T(8,128)}, u32[]{:S(2)}) %copy-start.1) | copy-done | bytes 139288
  24.6 2.9 %shard_map.69 = (f32[2,1024,256]{2,1,0:T(8,128)}, f32[2,1024]{1,0:T(2,128)}) custom-call(f32[136,256]{1,0:T(8,128)S(1)} %copy-done.1, f32[2,1024,256]{2,1,0:T(8,128)S(1)} %copy-done, f32[2,1024]{1,0:T(2,128)S(1)} %copy-done.2), custom_call_target="tpu_custom_call" | custom-call | tf_op jit(solution)/shard_map/pallas_call | solution.py:293
Async XLA Ops:
  0.6 23.1 %copy-start.2 = (f32[2,1024]{1,0:T(2,128)S(1)}, f32[2,1024]{1,0:T(2,128)}, u32[]{:S(2)}) copy-start(f32[2,1024]{1,0:T(2,128)} %accums_ref.1) | copy-start | bytes 24580
  0.6 23.1 %copy-start = (f32[2,1024,256]{2,1,0:T(8,128)S(1)}, f32[2,1024,256]{2,1,0:T(8,128)}, u32[]{:S(2)}) copy-start(f32[2,1024,256]{2,1,0:T(8,128)} %tables_ref.1) | copy-start | bytes 6291460
  23.7 0.9 %copy-start.1 = (f32[136,256]{1,0:T(8,128)S(1)}, f32[136,256]{1,0:T(8,128)}, u32[]{:S(2)}) copy-start(f32[136,256]{1,0:T(8,128)} %shard_map.68.packed_ref) | copy-start | bytes 417796
where the time goes:
time: 27.7 us; the launch traced here: 27.6 us
  Pallas kernels  26 us (94%)
  local copies, waits for them, and re-layouts  0.91 us (3%)
  between operations  0.68 us (2%)
    pallas_call x1, Pallas kernels, local_step(): pl.pallas_call(functools.partial(exchange_kernel, n_group, n_local, chunk...  23 us
    pallas_call x1, Pallas kernels, local_step(): pl.pallas_call(functools.partial(update_kernel, n_group, slots), out_shap...  2.94 us
    unnamed x6, local copies, waits for them, and re-layouts  0.91 us

commit v1 on v0

v1 whole, which is shorter than its diff:
```python
import functools

import jax
import jax.numpy as jnp
from jax import lax
from jax.experimental import pallas as pl
from jax.experimental.pallas import tpu as pltpu
from jax.sharding import PartitionSpec as P

learning_rate = 0.1
epsilon = 1e-08
MESH = pl.DeviceIdType.MESH
PIECES = 2
BLOCKS = 4


def split_bf16(x):
    high = x.astype(jnp.bfloat16)
    rest = x - high.astype(jnp.float32)
    middle = rest.astype(jnp.bfloat16)
    low = (rest - middle.astype(jnp.float32)).astype(jnp.bfloat16)
    return jnp.concatenate([high, middle, low], axis=0)


def exchange_kernel(
    n_group, n_local, chunk, grads_hbm, index_hbm, rows_hbm, tables_hbm, accums_hbm,
    parts_ref, onehot_ref, tables_ref, new_accums_ref,
    grads, index, rows, accums, sums, pair, relay, recv, rows_recv, acc, same_ref, hit_ref, old_ref,
    grad_sems, index_sem, rows_sem, tables_sem, accums_sem, pair_sems, relay_sems,
    pair_send_sem, send_sem, recv_sem, row_send_sem, row_recv_sem, near_sem, far_sem,
):
    group, local = lax.axis_index("group"), lax.axis_index("local")
    look, width = grads.shape
    capacity = sums.shape[2]
    slots = rows.shape[1]
    rows_dev = tables_hbm.shape[1]
    n_chunk = look // chunk
    peers = n_local // BLOCKS
    buckets = peers * n_group
    rows_block = buckets * capacity
    places = 2 + peers
    block_me, peer_me = local // peers, lax.rem(local, peers)
    half = block_me // 2
    inner = lax.rem(block_me + half, 2)
    near = block_me + 1 - 2 * lax.rem(block_me, 2)
    across = BLOCKS - 1 - block_me
    order = (BLOCKS - 1 - 3 * half, 2 - half, near, block_me)

    def signal_near(sem):
        for o in range(1, peers):
            pl.semaphore_signal(
                sem, inc=1, device_id={"group": group, "local": block_me * peers + lax.rem(peer_me + o, peers)},
                device_id_type=MESH,
            )
        pl.semaphore_signal(
            sem, inc=1, device_id={"group": group, "local": near * peers + peer_me}, device_id_type=MESH
        )

        @pl.when(inner == 1)
        def _():
            pl.semaphore_signal(
                sem, inc=1, device_id={"group": group, "local": across * peers + peer_me}, device_id_type=MESH
            )

        for o in range(1, n_group):
            pl.semaphore_signal(
                sem, inc=1, device_id={"group": lax.rem(group + o, n_group), "local": local}, device_id_type=MESH
            )

    met = peers - 1 + 1 + n_group - 1 + inner

    index_load = pltpu.make_async_copy(index_hbm, index, index_sem)
    rows_load = pltpu.make_async_copy(rows_hbm, rows, rows_sem)
    tables_load = pltpu.make_async_copy(tables_hbm, tables_ref, tables_sem)
    accums_load = pltpu.make_async_copy(accums_hbm, accums, accums_sem)

    def load(k):
        at = pl.ds(k * chunk, chunk)
        return pltpu.make_async_copy(grads_hbm.at[at], grads.at[at], grad_sems.at[k])

    index_load.start()
    for k in range(n_chunk):
        load(k).start()
    rows_load.start()
    accums_load.start()
    barrier = pltpu.get_barrier_semaphore()
    signal_near(barrier)

    def send_pair(step, o, h):
        to = order[step] * peers + lax.rem(peer_me + o, peers)
        return pltpu.make_async_remote_copy(
            src_ref=sums.at[to * n_group + h],
            dst_ref=pair.at[(step * n_group + h) * (peers - 1) + (peers - 1 - o)],
            send_sem=pair_send_sem, recv_sem=pair_sems.at[step * n_group + h],
            device_id={"group": group, "local": block_me * peers + lax.rem(peer_me + o, peers)},
            device_id_type=MESH,
        )

    def send_relay(step, h):
        return pltpu.make_async_remote_copy(
            src_ref=sums.at[(order[step] * peers + peer_me) * n_group + h], dst_ref=relay.at[step * n_group + h],
            send_sem=send_sem, recv_sem=relay_sems.at[step * n_group + h],
            device_id={"group": group, "local": near * peers + peer_me}, device_id_type=MESH,
        )

    def send_bucket(l, h, place):
        return pltpu.make_async_remote_copy(
            src_ref=sums.at[l * n_group + h], dst_ref=recv.at[group * places + place],
            send_sem=send_sem, recv_sem=recv_sem,
            device_id={"group": h, "local": l}, device_id_type=MESH,
        )

    def send_rows(h):
        return pltpu.make_async_remote_copy(
            src_ref=rows, dst_ref=rows_recv.at[group],
            send_sem=row_send_sem, recv_sem=row_recv_sem,
            device_id={"group": h, "local": local}, device_id_type=MESH,
        )

    def sum_part(step, start, stop):
        block = order[step]
        targets = lax.broadcasted_iota(jnp.int32, (rows_block, chunk), 0) + block * rows_block

        def body(k, c):
            if step == 0:
                load(k).wait()
            at = pl.ds(pl.multiple_of(k * chunk, chunk), chunk)
            onehot = jnp.concatenate(
                [jnp.where(index[t : t + 1, at] == targets, 1.0, 0.0).astype(jnp.bfloat16) for t in range(2)],
                axis=0,
            )
            acc[...] += jnp.dot(onehot, grads[at, :], preferred_element_type=jnp.float32)
            return c

        if start == 0:
            acc[...] = jnp.zeros_like(acc)
        lax.fori_loop(start, stop, body, 0)
        if stop == n_chunk:
            for t in range(2):
                sums[pl.ds(block * buckets, buckets), t] = acc[t * rows_block : (t + 1) * rows_block, :].reshape(
                    buckets, capacity, width
                )

    def start_pairs(step):
        def one(i, c):
            send_pair(step, 1 + i // n_group, lax.rem(group + lax.rem(i, n_group), n_group)).start()
            return c

        lax.fori_loop(0, (peers - 1) * n_group, one, 0)

    def add_pairs(step, h):
        first = (step * n_group + h) * (peers - 1)
        pltpu.make_async_remote_copy(
            src_ref=pair.at[pl.ds(first, peers - 1)], dst_ref=pair.at[pl.ds(first, peers - 1)],
            send_sem=pair_send_sem, recv_sem=pair_sems.at[step * n_group + h],
            device_id={"group": group, "local": local}, device_id_type=MESH,
        ).wait_recv()
        at = (order[step] * peers + peer_me) * n_group + h
        total = sums[at]
        for p in range(peers - 1):
            total = total + pair[first + p]
        sums[at] = total

    def pass_relay(step):
        def one(i, c):
            h = lax.rem(group + i, n_group)
            add_pairs(step, h)

            @pl.when(inner == 0)
            def _():
                send_relay(step, h).start()

            return c

        lax.fori_loop(0, n_group, one, 0)

    def finish_relay(step, h):
        @pl.when(inner == 1)
        def _():
            pltpu.make_async_remote_copy(
                src_ref=relay.at[step * n_group + h], dst_ref=relay.at[step * n_group + h],
                send_sem=send_sem, recv_sem=relay_sems.at[step * n_group + h],
                device_id={"group": group, "local": local}, device_id_type=MESH,
            ).wait_recv()
            to = order[step] * peers + peer_me
            sums[to * n_group + h] = sums[to * n_group + h] + relay[step * n_group + h]
            send_bucket(to, h, 0).start()

    index_load.wait()
    sum_part(0, 0, n_chunk)
    pl.semaphore_wait(barrier, met)
    start_pairs(0)
    signal_near(near_sem)
    tables_load.start()
    rows_load.wait()

    def row_step(o, c):
        send_rows(lax.rem(group + o, n_group)).start()
        return c

    lax.fori_loop(1, n_group, row_step, 0)
    sum_part(1, 0, n_chunk)
    start_pairs(1)
    pl.semaphore_wait(near_sem, met)

    @pl.when(inner == 1)
    def _():
        pl.semaphore_signal(
            far_sem, inc=1, device_id={"group": group, "local": across * peers + peer_me}, device_id_type=MESH
        )

    sum_part(2, 0, n_chunk)
    start_pairs(2)
    pass_relay(0)
    middle = n_chunk // 2
    if middle:
        sum_part(3, 0, middle)

    @pl.when(inner == 1)
    def _():
        pl.semaphore_wait(far_sem, 1)

    def finish_first(i, c):
        finish_relay(0, lax.rem(group + i, n_group))
        return c

    lax.fori_loop(0, n_group, finish_first, 0)
    pass_relay(1)
    sum_part(3, middle, n_chunk)

    def own_step(i, c):
        l = block_me * peers + lax.rem(peer_me + 1 + i // n_group, peers)
        send_bucket(l, lax.rem(group + 1 + i, n_group), 2 + peer_me).start()
        return c

    lax.fori_loop(0, buckets - 1, own_step, 0)
    recv[group * places + 2 + peer_me] = sums[local * n_group + group]

    def last_step(i, c):
        h = lax.rem(group + i, n_group)
        add_pairs(2, h)
        send_bucket(order[2] * peers + peer_me, h, 1).start()
        finish_relay(1, h)
        return c

    lax.fori_loop(0, n_group, last_step, 0)

    row_wait = pltpu.make_async_remote_copy(
        src_ref=rows_recv.at[pl.ds(0, n_group - 1)], dst_ref=rows_recv.at[pl.ds(0, n_group - 1)],
        send_sem=row_send_sem, recv_sem=row_recv_sem,
        device_id={"group": group, "local": local}, device_id_type=MESH,
    )
    rows_recv[group] = rows[...]
    row_wait.wait_recv()
    accums_load.wait()
    base = ((group * n_local + local) * rows_dev).astype(jnp.float32)
    slot_at = lax.broadcasted_iota(jnp.int32, (capacity, slots), 0)
    lane_at = lax.broadcasted_iota(jnp.int32, (capacity, slots), 1)
    first_at = lax.broadcasted_iota(jnp.int32, (slots, slots), 0)
    second_at = lax.broadcasted_iota(jnp.int32, (slots, slots), 1)
    row_lane = lax.broadcasted_iota(jnp.int32, (slots, rows_dev), 1).astype(jnp.float32)
    for t in range(2):
        columns = []
        for g in range(n_group):
            mine = lane_at == slot_at + group * capacity
            numbers = rows_recv[g, t : t + 1, :].astype(jnp.float32)
            columns.append(jnp.sum(jnp.where(mine, numbers, 0.0), axis=1, keepdims=True))
        column = jnp.concatenate(columns, axis=0)
        column = jnp.where(column < 0.0, -1.0, column - base)
        as_row = jnp.sum(jnp.where(first_at == second_at, column, 0.0), axis=0, keepdims=True)
        same = jnp.where(column == as_row, 1.0, 0.0)
        same_ref[t] = jnp.concatenate([same] * 3, axis=1).astype(jnp.bfloat16)
        hit = jnp.where(row_lane == column, 1.0, 0.0)
        hit_ref[t] = hit
        old_ref[t] = jnp.broadcast_to(jnp.sum(hit * accums[t : t + 1, :], axis=1, keepdims=True), old_ref.shape[1:])
        earlier = jnp.max(jnp.where(first_at < second_at, same, 0.0), axis=0, keepdims=True)
        target = jnp.where(earlier > 0.0, -1.0, as_row)
        target = jnp.concatenate([target] * 3, axis=1)
        piece = rows_dev // 8
        for i in range(8):
            piece_row = lax.broadcasted_iota(jnp.int32, (piece, 3 * slots), 0).astype(jnp.float32) + float(i * piece)
            onehot_ref[t, i * piece : (i + 1) * piece] = jnp.where(piece_row == target, 1.0, 0.0).astype(jnp.bfloat16)

    row_wait.wait_send()
    tables_load.wait()
    pair_parts = (BLOCKS - 1) * n_group * (peers - 1)
    pltpu.make_async_remote_copy(
        src_ref=pair.at[pl.ds(0, pair_parts)], dst_ref=pair.at[pl.ds(0, pair_parts)],
        send_sem=pair_send_sem, recv_sem=recv_sem,
        device_id={"group": group, "local": local}, device_id_type=MESH,
    ).wait_send()
    sent = (BLOCKS - 1) * n_group + buckets - 1
    pltpu.make_async_remote_copy(
        src_ref=sums.at[pl.ds(0, sent)], dst_ref=sums.at[pl.ds(0, sent)],
        send_sem=send_sem, recv_sem=recv_sem,
        device_id={"group": group, "local": local}, device_id_type=MESH,
    ).wait_send()
    parts = n_group * places - 1
    pltpu.make_async_remote_copy(
        src_ref=recv.at[pl.ds(0, parts)], dst_ref=recv.at[pl.ds(0, parts)],
        send_sem=send_sem, recv_sem=recv_sem,
        device_id={"group": group, "local": local}, device_id_type=MESH,
    ).wait_recv()
    for t in range(2):
        lists = []
        for g in range(n_group):
            total = recv[g * places, t]
            for p in range(1, places):
                total = total + recv[g * places + p, t]
            lists.append(total)
        totals = jnp.dot(
            same_ref[t], split_bf16(jnp.concatenate(lists, axis=0)), preferred_element_type=jnp.float32
        )
        squares = jnp.mean(totals * totals, axis=1, keepdims=True)
        added = jnp.max(hit_ref[t] * squares, axis=0, keepdims=True)
        new_accums_ref[t : t + 1, :] = accums[t : t + 1, :] + added
        change = learning_rate * totals / (jnp.sqrt(old_ref[t][:, 0:1] + squares) + epsilon)
        parts_ref[t] = split_bf16(change)


def update_kernel(parts_ref, onehot_ref, tables_ref, accums_ref, new_tables_hbm, new_accums_hbm, new, out_sems, accums_sem):
    rows_dev = tables_ref.shape[1]
    piece = rows_dev // PIECES
    accums_out = pltpu.make_async_copy(accums_ref, new_accums_hbm, accums_sem)
    accums_out.start()

    def out(t, i):
        at = pl.ds(i * piece, piece)
        return pltpu.make_async_copy(new.at[t, at], new_tables_hbm.at[t, at], out_sems.at[t, i])

    for t in range(2):
        for i in range(PIECES):
            at = slice(i * piece, (i + 1) * piece)
            new[t, at] = tables_ref[t, at] - jnp.dot(
                onehot_ref[t, at], parts_ref[t], preferred_element_type=jnp.float32
            )
            out(t, i).start()
    accums_out.wait()
    for t in range(2):
        for i in range(PIECES):
            out(t, i).wait()


def local_step(n_group, n_local, lookup_grads, slot_index, unique_rows, tables, accums):
    look, width = lookup_grads.shape
    slots = unique_rows.shape[1]
    capacity = slots // n_group
    n_dev = n_group * n_local
    rows_dev = tables.shape[1]
    chunk = min(4096, look)
    peers = n_local // BLOCKS
    block_rows = 2 * (slots * n_local // BLOCKS)
    vmem = pl.BlockSpec(memory_space=pltpu.VMEM)
    hbm = pl.BlockSpec(memory_space=pltpu.HBM)
    dma = pltpu.SemaphoreType.DMA
    regular = pltpu.SemaphoreType.REGULAR
    prepared = pl.pallas_call(
        functools.partial(exchange_kernel, n_group, n_local, chunk),
        out_shape=(
            pltpu.VMEM((2, 3 * slots, width), jnp.bfloat16),
            pltpu.VMEM((2, rows_dev, 3 * slots), jnp.bfloat16),
            pltpu.VMEM(tables.shape, jnp.float32),
            pltpu.VMEM(accums.shape, jnp.float32),
        ),
        in_specs=[hbm] * 5,
        out_specs=(vmem, vmem, vmem, vmem),
        scratch_shapes=[
            pltpu.VMEM((look, width), jnp.bfloat16),
            pltpu.VMEM((2, look), jnp.int32),
            pltpu.VMEM((2, slots), jnp.int32),
            pltpu.VMEM((2, rows_dev), jnp.float32),
            pltpu.VMEM((n_dev, 2, capacity, width), jnp.float32),
            pltpu.VMEM(((BLOCKS - 1) * n_group * (peers - 1), 2, capacity, width), jnp.float32),
            pltpu.VMEM((2 * n_group, 2, capacity, width), jnp.float32),
            pltpu.VMEM((n_group * (2 + peers), 2, capacity, width), jnp.float32),
            pltpu.VMEM((n_group, 2, slots), jnp.int32),
            pltpu.VMEM((block_rows, width), jnp.float32),
            pltpu.VMEM((2, slots, 3 * slots), jnp.bfloat16),
            pltpu.VMEM((2, slots, rows_dev), jnp.float32),
            pltpu.VMEM((2, slots, 128), jnp.float32),
            dma((look // chunk,)), dma, dma, dma, dma,
            dma(((BLOCKS - 1) * n_group,)), dma((2 * n_group,)),
            dma, dma, dma, dma, dma, regular, regular,
        ],
        compiler_params=pltpu.CompilerParams(
            collective_id=0, has_side_effects=True, vmem_limit_bytes=48 * 2**20
        ),
        cost_estimate=pl.CostEstimate(flops=2 * 2 * look * width * slots * n_local, bytes_accessed=2 * look * width, transcendentals=0),
    )(*[pltpu.with_memory_space_constraint(x, pltpu.HBM) for x in (lookup_grads, slot_index, unique_rows, tables, accums)])
    return pl.pallas_call(
        update_kernel,
        out_shape=(
            jax.ShapeDtypeStruct(tables.shape, jnp.float32),
            jax.ShapeDtypeStruct(accums.shape, jnp.float32),
        ),
        in_specs=[vmem] * 4,
        out_specs=(hbm, hbm),
        scratch_shapes=[
            pltpu.VMEM((2, rows_dev, width), jnp.float32),
            dma((2, PIECES)), dma,
        ],
        compiler_params=pltpu.CompilerParams(vmem_limit_bytes=16 * 2**20),
    )(*prepared)


def solution(mesh):
    n_group, n_local = mesh.shape["group"], mesh.shape["local"]
    return jax.shard_map(
        functools.partial(local_step, n_group, n_local),
        mesh=mesh,
        in_specs=(
            P(("group", "local"), None),
            P(None, ("group", "local")),
            P(None, ("group", "local")),
            P(None, ("group", "local"), None),
            P(None, ("group", "local")),
        ),
        out_specs=(P(None, ("group", "local"), None), P(None, ("group", "local"))),
        check_vma=False,
    )
```

time: 27.7 us -> 23.6 us (0.85)
  Pallas kernels: 26 us -> 22.8 us
  local copies, waits for them, and re-layouts: 0.91 us -> 0 us
    pallas_call x1, Pallas kernels: 23 us -> 21.2 us  [local_step(): pl.pallas_call(functools.partial(exchange_kernel, n_group, n_local, chunk...]
    pallas_call x1, Pallas kernels: 2.94 us -> 1.66 us  [local_step(): pl.pallas_call(update_kernel, out_shape=(jax.ShapeDtypeStruct(tables.shap...]
    unnamed x6 -> x0, local copies, waits for them, and re-layouts: 0.91 us -> none
where the time goes in v1:
time: 23.6 us; the launch traced here: 23.5 us
  Pallas kernels  22.8 us (97%)
  between operations  0.64 us (3%)
    pallas_call x1, Pallas kernels, local_step(): pl.pallas_call(functools.partial(exchange_kernel, n_group, n_local, chunk...  21.2 us
    pallas_call x1, Pallas kernels, local_step(): pl.pallas_call(update_kernel, out_shape=(jax.ShapeDtypeStruct(tables.shap...  1.66 us

profile of v1, /device:TPU:0, one launch (start us, length us, event | category | flops | bytes accessed | tf_op | source)
XLA Modules:
  0.0 23.5 jit_solution(16625916381503574909)
XLA Ops:
  0.6 21.2 %shard_map.68 = (bf16[2,192,256]{2,1,0:T(8,128)(2,1)S(1)}, bf16[2,1024,192]{2,1,0:T(8,128)(2,1)S(1)}, f32[2,1024,256]{2,1,0:T(8,128)S(1)}, f32[2,1024]{1,0:T(2,128)S(1)}) custom-call(bf16[8192,256]{1,0:T(8,128)(2,1)} %grads_hbm.1, s32[2,8192]{1,0:T(2,128)} %index_hbm.1, s32[2,64]{1,0:T(2,128)} %rows_hbm.1, f32[2,1024,256]{2,1,0:T(8,128)} %tables_hbm.1, ...), custom_call_target="tpu_custom_call" | custom-call | flops 4294967296 | bytes 4194304 | tf_op jit(solution)/shard_map/pallas_call | solution.py:357
  21.8 1.7 %shard_map.69 = (f32[2,1024,256]{2,1,0:T(8,128)}, f32[2,1024]{1,0:T(2,128)}) custom-call(bf16[2,192,256]{2,1,0:T(8,128)(2,1)S(1)} %get-tuple-element.6.parts_ref, bf16[2,1024,192]{2,1,0:T(8,128)(2,1)S(1)} %get-tuple-element.7.onehot_ref, f32[2,1024,256]{2,1,0:T(8,128)S(1)} %get-tuple-element.8.tables_ref, f32[2,1024]{1,0:T(2,128)S(1)} %get-tuple-element.9.accums_ref), custom_call_target="tpu_custom_call" | custom-call | tf_op jit(solution)/shard_map/pallas_call | solution.py:390

commit v2 on v1

--- a/solution.py
+++ b/solution.py
@@ -23,28 +23,30 @@
 
 
 def exchange_kernel(
-    n_group, n_local, chunk, grads_hbm, index_hbm, rows_hbm, tables_hbm, accums_hbm,
+    n_group, n_local, grads_hbm, index_hbm, rows_hbm, tables_hbm, accums_hbm,
     parts_ref, onehot_ref, tables_ref, new_accums_ref,
-    grads, index, rows, accums, sums, pair, relay, recv, rows_recv, acc, same_ref, hit_ref, old_ref,
-    grad_sems, index_sem, rows_sem, tables_sem, accums_sem, pair_sems, relay_sems,
+    grads, index, rows, accums, sums, pair, relay, recv, rows_recv, same_ref, hit_ref, old_ref,
+    grads_sem, index_sem, rows_sem, tables_sem, accums_sem, pair_sems, relay_sems,
     pair_send_sem, send_sem, recv_sem, row_send_sem, row_recv_sem, near_sem, far_sem,
 ):
     group, local = lax.axis_index("group"), lax.axis_index("local")
-    look, width = grads.shape
+    width = grads.shape[1]
     capacity = sums.shape[2]
     slots = rows.shape[1]
     rows_dev = tables_hbm.shape[1]
-    n_chunk = look // chunk
     peers = n_local // BLOCKS
     buckets = peers * n_group
-    rows_block = buckets * capacity
-    places = 2 + peers
+    early = n_group // 2
+    places = 3 + peers
     block_me, peer_me = local // peers, lax.rem(local, peers)
     half = block_me // 2
     inner = lax.rem(block_me + half, 2)
     near = block_me + 1 - 2 * lax.rem(block_me, 2)
     across = BLOCKS - 1 - block_me
-    order = (BLOCKS - 1 - 3 * half, 2 - half, near, block_me)
+    far_inner, far_outer = 2 - half, BLOCKS - 1 - 3 * half
+    order = (
+        far_outer + inner * (far_inner - far_outer), far_inner + inner * (far_outer - far_inner), near, block_me
+    )
 
     def signal_near(sem):
         for o in range(1, peers):
@@ -74,13 +76,10 @@
     tables_load = pltpu.make_async_copy(tables_hbm, tables_ref, tables_sem)
     accums_load = pltpu.make_async_copy(accums_hbm, accums, accums_sem)
 
-    def load(k):
-        at = pl.ds(k * chunk, chunk)
-        return pltpu.make_async_copy(grads_hbm.at[at], grads.at[at], grad_sems.at[k])
+    grads_load = pltpu.make_async_copy(grads_hbm, grads, grads_sem)
 
     index_load.start()
-    for k in range(n_chunk):
-        load(k).start()
+    grads_load.start()
     rows_load.start()
     accums_load.start()
     barrier = pltpu.get_barrier_semaphore()
@@ -96,10 +95,10 @@
             device_id_type=MESH,
         )
 
-    def send_relay(step, h):
+    def send_relay(h):
         return pltpu.make_async_remote_copy(
-            src_ref=sums.at[(order[step] * peers + peer_me) * n_group + h], dst_ref=relay.at[step * n_group + h],
-            send_sem=send_sem, recv_sem=relay_sems.at[step * n_group + h],
+            src_ref=sums.at[(order[0] * peers + peer_me) * n_group + h], dst_ref=relay.at[h],
+            send_sem=send_sem, recv_sem=relay_sems.at[h],
             device_id={"group": group, "local": near * peers + peer_me}, device_id_type=MESH,
         )
 
@@ -117,33 +116,35 @@
             device_id={"group": h, "local": local}, device_id_type=MESH,
         )
 
-    def sum_part(step, start, stop):
-        block = order[step]
-        targets = lax.broadcasted_iota(jnp.int32, (rows_block, chunk), 0) + block * rows_block
-
-        def body(k, c):
-            if step == 0:
-                load(k).wait()
-            at = pl.ds(pl.multiple_of(k * chunk, chunk), chunk)
-            onehot = jnp.concatenate(
-                [jnp.where(index[t : t + 1, at] == targets, 1.0, 0.0).astype(jnp.bfloat16) for t in range(2)],
-                axis=0,
-            )
-            acc[...] += jnp.dot(onehot, grads[at, :], preferred_element_type=jnp.float32)
-            return c
-
-        if start == 0:
-            acc[...] = jnp.zeros_like(acc)
-        lax.fori_loop(start, stop, body, 0)
-        if stop == n_chunk:
-            for t in range(2):
-                sums[pl.ds(block * buckets, buckets), t] = acc[t * rows_block : (t + 1) * rows_block, :].reshape(
-                    buckets, capacity, width
-                )
+    def whole(block, o):
+        at = (block * peers + lax.rem(peer_me + o, peers)) * n_group
+        return at, at + early
+
+    runs, events = [], {}
+
+    def sum_runs(q):
+        first, second = (
+            functools.reduce(lambda x, k: jnp.where(q == k, runs[k][i], x), range(1, len(runs)), runs[0][i])
+            for i in range(2)
+        )
+        row = lax.broadcasted_iota(jnp.int32, (early * capacity, 1), 0)
+        targets = jnp.concatenate([row + first * capacity, row + second * capacity], axis=0)
+        onehot = jnp.concatenate(
+            [jnp.where(index[t : t + 1, :] == targets, 1.0, 0.0).astype(jnp.bfloat16) for t in range(2)], axis=0
+        )
+        total = jnp.dot(onehot, grads[...], preferred_element_type=jnp.float32)
+        n_rows = early * capacity
+        for t in range(2):
+            for i, at in enumerate((first, second)):
+                start = (2 * t + i) * n_rows
+                sums[pl.ds(at, early), t] = total[start : start + n_rows, :].reshape(early, capacity, width)
+
+    def turn(step, i):
+        return jnp.where(order[step] == 0, i, lax.rem(i + 1, 2) * early + i // 2)
 
     def start_pairs(step):
         def one(i, c):
-            send_pair(step, 1 + i // n_group, lax.rem(group + lax.rem(i, n_group), n_group)).start()
+            send_pair(step, 1 + i // n_group, turn(step, lax.rem(i, n_group))).start()
             return c
 
         lax.fori_loop(0, (peers - 1) * n_group, one, 0)
@@ -161,89 +162,125 @@
             total = total + pair[first + p]
         sums[at] = total
 
-    def pass_relay(step):
-        def one(i, c):
-            h = lax.rem(group + i, n_group)
-            add_pairs(step, h)
-
-            @pl.when(inner == 0)
-            def _():
-                send_relay(step, h).start()
-
-            return c
-
-        lax.fori_loop(0, n_group, one, 0)
-
-    def finish_relay(step, h):
+    def pass_on(step, h, place):
+        send_bucket(order[step] * peers + peer_me, h, place).start()
+
+    def pass_first(h):
+        add_pairs(0, h)
+        pl.when(inner == 0)(lambda: send_relay(h).start())
+        pl.when(inner == 1)(lambda: pass_on(0, h, 0))
+
+    def pass_second(h):
+        add_pairs(1, h)
+
         @pl.when(inner == 1)
         def _():
             pltpu.make_async_remote_copy(
-                src_ref=relay.at[step * n_group + h], dst_ref=relay.at[step * n_group + h],
-                send_sem=send_sem, recv_sem=relay_sems.at[step * n_group + h],
+                src_ref=relay.at[h], dst_ref=relay.at[h], send_sem=send_sem, recv_sem=relay_sems.at[h],
                 device_id={"group": group, "local": local}, device_id_type=MESH,
             ).wait_recv()
-            to = order[step] * peers + peer_me
-            sums[to * n_group + h] = sums[to * n_group + h] + relay[step * n_group + h]
-            send_bucket(to, h, 0).start()
+            at = (order[1] * peers + peer_me) * n_group + h
+            sums[at] = sums[at] + relay[h]
+
+        pass_on(1, h, 2 - 2 * inner)
+
+    def pass_third(h):
+        add_pairs(2, h)
+        pass_on(2, h, 1)
+
+    def for_groups(step, action, start=0, stop=n_group):
+        def one(i, c):
+            action(turn(step, i))
+            return c
+
+        lax.fori_loop(start, stop, one, 0)
+
+    @pl.when(inner == 0)
+    def _():
+        for g in range(n_group):
+            recv[g * places + 2] = jnp.zeros(recv.shape[1:], jnp.float32)
+
+    def open_up():
+        pl.semaphore_wait(barrier, met)
+        start_pairs(0)
+        signal_near(near_sem)
+        tables_load.start()
+        rows_load.wait()
+
+        def row_step(o, c):
+            send_rows(lax.rem(group + o, n_group)).start()
+            return c
+
+        lax.fori_loop(1, n_group, row_step, 0)
+
+    def meet_far():
+        pl.semaphore_wait(near_sem, met)
+        pl.semaphore_signal(
+            far_sem, inc=1, device_id={"group": group, "local": near * peers + peer_me}, device_id_type=MESH
+        )
+
+        @pl.when(inner == 1)
+        def _():
+            pl.semaphore_signal(
+                far_sem, inc=1, device_id={"group": group, "local": across * peers + peer_me}, device_id_type=MESH
+            )
+
+    def stay():
+        def stay_step(h):
+            pl.when(h != group)(lambda: send_bucket(local, h, 3 + peer_me).start())
+
+        for_groups(3, stay_step)
+        recv[group * places + 3 + peer_me] = sums[local * n_group + group]
+
+    def own():
+        def own_step(i, c):
+            l = block_me * peers + lax.rem(peer_me + 1 + i // n_group, peers)
+            send_bucket(l, turn(3, lax.rem(i, n_group)), 3 + peer_me).start()
+            return c
+
+        lax.fori_loop(0, (peers - 1) * n_group, own_step, 0)
+
+    def relay_some(start, stop, late):
+        pl.when(lax.rem(group, 2) != late)(lambda: for_groups(0, pass_first, start, stop))
+
+    def add_runs(block, o, *actions):
+        runs.append(whole(block, o))
+        events[len(runs) - 1] = actions
+
+    def add_peers(block, *actions):
+        for o in range(1, peers):
+            add_runs(block, o, *(actions if o == peers - 1 else ()))
+
+    first_half, second_half = (0, early), (early, n_group)
+    add_peers(order[0], open_up)
+    add_runs(order[3], 0, stay)
+    add_runs(order[0], 0)
+    add_peers(order[1], lambda: start_pairs(1), meet_far, lambda: relay_some(*first_half, 0))
+    add_runs(order[1], 0, lambda: relay_some(*second_half, 0), lambda: relay_some(*first_half, 1))
+    add_peers(order[2], lambda: start_pairs(2))
+    add_runs(order[2], 0, lambda: relay_some(*second_half, 1))
+    add_peers(order[3], own)
 
     index_load.wait()
-    sum_part(0, 0, n_chunk)
-    pl.semaphore_wait(barrier, met)
-    start_pairs(0)
-    signal_near(near_sem)
-    tables_load.start()
-    rows_load.wait()
-
-    def row_step(o, c):
-        send_rows(lax.rem(group + o, n_group)).start()
+    grads_load.wait()
+
+    def sum_step(q, c):
+        sum_runs(q)
+        for k, actions in events.items():
+
+            @pl.when(q == k)
+            def _():
+                for action in actions:
+                    action()
+
         return c
 
-    lax.fori_loop(1, n_group, row_step, 0)
-    sum_part(1, 0, n_chunk)
-    start_pairs(1)
-    pl.semaphore_wait(near_sem, met)
-
-    @pl.when(inner == 1)
-    def _():
-        pl.semaphore_signal(
-            far_sem, inc=1, device_id={"group": group, "local": across * peers + peer_me}, device_id_type=MESH
-        )
-
-    sum_part(2, 0, n_chunk)
-    start_pairs(2)
-    pass_relay(0)
-    middle = n_chunk // 2
-    if middle:
-        sum_part(3, 0, middle)
-
-    @pl.when(inner == 1)
-    def _():
-        pl.semaphore_wait(far_sem, 1)
-
-    def finish_first(i, c):
-        finish_relay(0, lax.rem(group + i, n_group))
-        return c
-
-    lax.fori_loop(0, n_group, finish_first, 0)
-    pass_relay(1)
-    sum_part(3, middle, n_chunk)
-
-    def own_step(i, c):
-        l = block_me * peers + lax.rem(peer_me + 1 + i // n_group, peers)
-        send_bucket(l, lax.rem(group + 1 + i, n_group), 2 + peer_me).start()
-        return c
-
-    lax.fori_loop(0, buckets - 1, own_step, 0)
-    recv[group * places + 2 + peer_me] = sums[local * n_group + group]
-
-    def last_step(i, c):
-        h = lax.rem(group + i, n_group)
-        add_pairs(2, h)
-        send_bucket(order[2] * peers + peer_me, h, 1).start()
-        finish_relay(1, h)
-        return c
-
-    lax.fori_loop(0, n_group, last_step, 0)
+    lax.fori_loop(0, len(runs), sum_step, 0)
+
+    pl.semaphore_wait(far_sem, 1 + inner)
+
+    for_groups(1, pass_second)
+    for_groups(2, pass_third)
 
     row_wait = pltpu.make_async_remote_copy(
         src_ref=rows_recv.at[pl.ds(0, n_group - 1)], dst_ref=rows_recv.at[pl.ds(0, n_group - 1)],
@@ -295,12 +332,15 @@
         send_sem=send_sem, recv_sem=recv_sem,
         device_id={"group": group, "local": local}, device_id_type=MESH,
     ).wait_send()
-    parts = n_group * places - 1
-    pltpu.make_async_remote_copy(
-        src_ref=recv.at[pl.ds(0, parts)], dst_ref=recv.at[pl.ds(0, parts)],
-        send_sem=send_sem, recv_sem=recv_sem,
-        device_id={"group": group, "local": local}, device_id_type=MESH,
-    ).wait_recv()
+    def wait_parts(n):
+        pltpu.make_async_remote_copy(
+            src_ref=recv.at[pl.ds(0, n)], dst_ref=recv.at[pl.ds(0, n)],
+            send_sem=send_sem, recv_sem=recv_sem,
+            device_id={"group": group, "local": local}, device_id_type=MESH,
+        ).wait_recv()
+
+    pl.when(inner == 0)(lambda: wait_parts(n_group * (places - 1) - 1))
+    pl.when(inner == 1)(lambda: wait_parts(n_group * places - 1))
     for t in range(2):
         lists = []
         for g in range(n_group):
@@ -328,13 +368,14 @@
         at = pl.ds(i * piece, piece)
         return pltpu.make_async_copy(new.at[t, at], new_tables_hbm.at[t, at], out_sems.at[t, i])
 
-    for t in range(2):
-        for i in range(PIECES):
-            at = slice(i * piece, (i + 1) * piece)
-            new[t, at] = tables_ref[t, at] - jnp.dot(
-                onehot_ref[t, at], parts_ref[t], preferred_element_type=jnp.float32
-            )
-            out(t, i).start()
+    def step(k, c):
+        t, i = k // PIECES, lax.rem(k, PIECES)
+        at = pl.ds(pl.multiple_of(i * piece, piece), piece)
+        new[t, at] = tables_ref[t, at] - jnp.dot(onehot_ref[t, at], parts_ref[t], preferred_element_type=jnp.float32)
+        out(t, i).start()
+        return c
+
+    lax.fori_loop(0, 2 * PIECES, step, 0)
     accums_out.wait()
     for t in range(2):
         for i in range(PIECES):
@@ -347,15 +388,13 @@
     capacity = slots // n_group
     n_dev = n_group * n_local
     rows_dev = tables.shape[1]
-    chunk = min(4096, look)
     peers = n_local // BLOCKS
-    block_rows = 2 * (slots * n_local // BLOCKS)
     vmem = pl.BlockSpec(memory_space=pltpu.VMEM)
     hbm = pl.BlockSpec(memory_space=pltpu.HBM)
     dma = pltpu.SemaphoreType.DMA
     regular = pltpu.SemaphoreType.REGULAR
     prepared = pl.pallas_call(
-        functools.partial(exchange_kernel, n_group, n_local, chunk),
+        functools.partial(exchange_kernel, n_group, n_local),
         out_shape=(
             pltpu.VMEM((2, 3 * slots, width), jnp.bfloat16),
             pltpu.VMEM((2, rows_dev, 3 * slots), jnp.bfloat16),
@@ -371,15 +410,14 @@
             pltpu.VMEM((2, rows_dev), jnp.float32),
             pltpu.VMEM((n_dev, 2, capacity, width), jnp.float32),
             pltpu.VMEM(((BLOCKS - 1) * n_group * (peers - 1), 2, capacity, width), jnp.float32),
-            pltpu.VMEM((2 * n_group, 2, capacity, width), jnp.float32),
-            pltpu.VMEM((n_group * (2 + peers), 2, capacity, width), jnp.float32),
+            pltpu.VMEM((n_group, 2, capacity, width), jnp.float32),
+            pltpu.VMEM((n_group * (3 + peers), 2, capacity, width), jnp.float32),
             pltpu.VMEM((n_group, 2, slots), jnp.int32),
-            pltpu.VMEM((block_rows, width), jnp.float32),
             pltpu.VMEM((2, slots, 3 * slots), jnp.bfloat16),
             pltpu.VMEM((2, slots, rows_dev), jnp.float32),
             pltpu.VMEM((2, slots, 128), jnp.float32),
-            dma((look // chunk,)), dma, dma, dma, dma,
-            dma(((BLOCKS - 1) * n_group,)), dma((2 * n_group,)),
+            dma, dma, dma, dma, dma,
+            dma(((BLOCKS - 1) * n_group,)), dma((n_group,)),
             dma, dma, dma, dma, dma, regular, regular,
         ],
         compiler_params=pltpu.CompilerParams(

time: 23.6 us -> 23.6 us (level); the launches traced: 23.5 us -> 23.2 us
    pallas_call x1, Pallas kernels: 21.2 us -> 20.8 us  [local_step(): pl.pallas_call(functools.partial(exchange_kernel, n_group, n_local), out_...]
where the time goes in v2:
time: 23.6 us; the launch traced here: 23.2 us
  Pallas kernels  22.6 us (96%)
  between operations  0.64 us (3%)
    pallas_call x1, Pallas kernels, local_step(): pl.pallas_call(functools.partial(exchange_kernel, n_group, n_local), out_...  20.8 us
    pallas_call x1, Pallas kernels, local_step(): pl.pallas_call(update_kernel, out_shape=(jax.ShapeDtypeStruct(tables.shap...  1.75 us

profile of v2, /device:TPU:0, one launch (start us, length us, event | category | flops | bytes accessed | tf_op | source)
XLA Modules:
  0.0 23.2 jit_solution(2838131050274597166)
XLA Ops:
  0.6 20.8 %shard_map.68 = (bf16[2,192,256]{2,1,0:T(8,128)(2,1)S(1)}, bf16[2,1024,192]{2,1,0:T(8,128)(2,1)S(1)}, f32[2,1024,256]{2,1,0:T(8,128)S(1)}, f32[2,1024]{1,0:T(2,128)S(1)}) custom-call(bf16[8192,256]{1,0:T(8,128)(2,1)} %grads_hbm.1, s32[2,8192]{1,0:T(2,128)} %index_hbm.1, s32[2,64]{1,0:T(2,128)} %rows_hbm.1, f32[2,1024,256]{2,1,0:T(8,128)} %tables_hbm.1, ...), custom_call_target="tpu_custom_call" | custom-call | flops 4294967296 | bytes 4194304 | tf_op jit(solution)/shard_map/pallas_call | solution.py:396
  21.5 1.8 %shard_map.69 = (f32[2,1024,256]{2,1,0:T(8,128)}, f32[2,1024]{1,0:T(2,128)}) custom-call(bf16[2,192,256]{2,1,0:T(8,128)(2,1)S(1)} %get-tuple-element.6.parts_ref, bf16[2,1024,192]{2,1,0:T(8,128)(2,1)S(1)} %get-tuple-element.7.onehot_ref, f32[2,1024,256]{2,1,0:T(8,128)S(1)} %get-tuple-element.8.tables_ref, f32[2,1024]{1,0:T(2,128)S(1)} %get-tuple-element.9.accums_ref), custom_call_target="tpu_custom_call" | custom-call | tf_op jit(solution)/shard_map/pallas_call | solution.py:428

commit v3 on v2

--- a/solution.py
+++ b/solution.py
@@ -10,7 +10,7 @@
 learning_rate = 0.1
 epsilon = 1e-08
 MESH = pl.DeviceIdType.MESH
-PIECES = 2
+PIECES = 4
 BLOCKS = 4
 
 
@@ -25,8 +25,8 @@
 def exchange_kernel(
     n_group, n_local, grads_hbm, index_hbm, rows_hbm, tables_hbm, accums_hbm,
     parts_ref, onehot_ref, tables_ref, new_accums_ref,
-    grads, index, rows, accums, sums, pair, relay, recv, rows_recv, same_ref, hit_ref, old_ref,
-    grads_sem, index_sem, rows_sem, tables_sem, accums_sem, pair_sems, relay_sems,
+    grads, index, rows, accums, sums, pair, relay, raw, recv, rows_recv, same_ref, hit_ref, old_ref,
+    grads_sems, index_sem, rows_sem, tables_sem, accums_sem, pair_sems, relay_sems, raw_sem,
     pair_send_sem, send_sem, recv_sem, row_send_sem, row_recv_sem, near_sem, far_sem,
 ):
     group, local = lax.axis_index("group"), lax.axis_index("local")
@@ -76,10 +76,15 @@
     tables_load = pltpu.make_async_copy(tables_hbm, tables_ref, tables_sem)
     accums_load = pltpu.make_async_copy(accums_hbm, accums, accums_sem)
 
-    grads_load = pltpu.make_async_copy(grads_hbm, grads, grads_sem)
+    look = grads.shape[0]
+    halves_at = pl.ds(0, look // 2), pl.ds(look // 2, look - look // 2)
+    grads_loads = [
+        pltpu.make_async_copy(grads_hbm.at[at], grads.at[at], grads_sems.at[k]) for k, at in enumerate(halves_at)
+    ]
 
     index_load.start()
-    grads_load.start()
+    for grads_load in grads_loads:
+        grads_load.start()
     rows_load.start()
     accums_load.start()
     barrier = pltpu.get_barrier_semaphore()
@@ -120,34 +125,72 @@
         at = (block * peers + lax.rem(peer_me + o, peers)) * n_group
         return at, at + early
 
+    def halves(p, h):
+        at = (near * peers + p) * n_group + h
+        return at, at + n_group
+
     runs, events = [], {}
 
-    def sum_runs(q):
+    def sum_runs(q, cuts, ready=None):
         first, second = (
             functools.reduce(lambda x, k: jnp.where(q == k, runs[k][i], x), range(1, len(runs)), runs[0][i])
             for i in range(2)
         )
-        row = lax.broadcasted_iota(jnp.int32, (early * capacity, 1), 0)
+        n_rows = early * capacity
+        row = lax.broadcasted_iota(jnp.int32, (n_rows, 1), 0)
         targets = jnp.concatenate([row + first * capacity, row + second * capacity], axis=0)
-        onehot = jnp.concatenate(
-            [jnp.where(index[t : t + 1, :] == targets, 1.0, 0.0).astype(jnp.bfloat16) for t in range(2)], axis=0
-        )
-        total = jnp.dot(onehot, grads[...], preferred_element_type=jnp.float32)
-        n_rows = early * capacity
+        total = None
+        for k, at in enumerate(cuts):
+            if ready is not None:
+                ready[k].wait()
+            onehot = jnp.concatenate(
+                [jnp.where(index[t : t + 1, at] == targets, 1.0, 0.0).astype(jnp.bfloat16) for t in range(2)], axis=0
+            )
+            part = jnp.dot(onehot, grads[at, :], preferred_element_type=jnp.float32)
+            total = part if total is None else total + part
         for t in range(2):
             for i, at in enumerate((first, second)):
                 start = (2 * t + i) * n_rows
                 sums[pl.ds(at, early), t] = total[start : start + n_rows, :].reshape(early, capacity, width)
 
-    def turn(step, i):
-        return jnp.where(order[step] == 0, i, lax.rem(i + 1, 2) * early + i // 2)
-
     def start_pairs(step):
         def one(i, c):
-            send_pair(step, 1 + i // n_group, turn(step, lax.rem(i, n_group))).start()
+            send_pair(step, 1 + i // n_group, lax.rem(i, n_group)).start()
             return c
 
         lax.fori_loop(0, (peers - 1) * n_group, one, 0)
+
+    def start_third():
+        def one(i, c):
+            send_pair(2, 1 + i // early, lax.rem(i, early)).start()
+            return c
+
+        lax.fori_loop(0, (peers - 1) * early, one, 0)
+
+    def send_raw():
+        def one(p, c):
+            pltpu.make_async_remote_copy(
+                src_ref=sums.at[pl.ds((near * peers + p) * n_group + early, n_group - early)],
+                dst_ref=raw.at[pl.ds(p * (n_group - early), n_group - early)],
+                send_sem=send_sem, recv_sem=raw_sem,
+                device_id={"group": group, "local": near * peers + peer_me}, device_id_type=MESH,
+            ).start()
+            return c
+
+        lax.fori_loop(0, peers, one, 0)
+
+    def add_raw():
+        pltpu.make_async_remote_copy(
+            src_ref=raw, dst_ref=raw, send_sem=send_sem, recv_sem=raw_sem,
+            device_id={"group": group, "local": local}, device_id_type=MESH,
+        ).wait_recv()
+
+        def one(p, c):
+            at = pl.ds((block_me * peers + p) * n_group + early, n_group - early)
+            sums[at] = sums[at] + raw[pl.ds(p * (n_group - early), n_group - early)]
+            return c
+
+        lax.fori_loop(0, peers, one, 0)
 
     def add_pairs(step, h):
         first = (step * n_group + h) * (peers - 1)
@@ -188,9 +231,9 @@
         add_pairs(2, h)
         pass_on(2, h, 1)
 
-    def for_groups(step, action, start=0, stop=n_group):
-        def one(i, c):
-            action(turn(step, i))
+    def for_groups(action, start=0, stop=n_group):
+        def one(h, c):
+            action(h)
             return c
 
         lax.fori_loop(start, stop, one, 0)
@@ -199,6 +242,11 @@
     def _():
         for g in range(n_group):
             recv[g * places + 2] = jnp.zeros(recv.shape[1:], jnp.float32)
+
+    @pl.when(group >= early)
+    def _():
+        for g in range(n_group):
+            recv[g * places + 1] = jnp.zeros(recv.shape[1:], jnp.float32)
 
     def open_up():
         pl.semaphore_wait(barrier, met)
@@ -225,62 +273,78 @@
                 far_sem, inc=1, device_id={"group": group, "local": across * peers + peer_me}, device_id_type=MESH
             )
 
-    def stay():
-        def stay_step(h):
+    def stay(start, stop):
+        def one(h, c):
             pl.when(h != group)(lambda: send_bucket(local, h, 3 + peer_me).start())
-
-        for_groups(3, stay_step)
-        recv[group * places + 3 + peer_me] = sums[local * n_group + group]
-
-    def own():
-        def own_step(i, c):
-            l = block_me * peers + lax.rem(peer_me + 1 + i // n_group, peers)
-            send_bucket(l, turn(3, lax.rem(i, n_group)), 3 + peer_me).start()
-            return c
-
-        lax.fori_loop(0, (peers - 1) * n_group, own_step, 0)
+            return c
+
+        lax.fori_loop(start, stop, one, 0)
+
+        @pl.when((group >= start) & (group < stop))
+        def _():
+            recv[group * places + 3 + peer_me] = sums[local * n_group + group]
+
+    def own(start, stop):
+        def one(i, c):
+            l = block_me * peers + lax.rem(peer_me + 1 + i // (stop - start), peers)
+            send_bucket(l, start + lax.rem(i, stop - start), 3 + peer_me).start()
+            return c
+
+        lax.fori_loop(0, (peers - 1) * (stop - start), one, 0)
 
     def relay_some(start, stop, late):
-        pl.when(lax.rem(group, 2) != late)(lambda: for_groups(0, pass_first, start, stop))
-
-    def add_runs(block, o, *actions):
-        runs.append(whole(block, o))
+        pl.when(lax.rem(group, 2) != late)(lambda: for_groups(pass_first, start, stop))
+
+    def add_runs(run, *actions):
+        runs.append(run)
         events[len(runs) - 1] = actions
 
     def add_peers(block, *actions):
         for o in range(1, peers):
-            add_runs(block, o, *(actions if o == peers - 1 else ()))
+            add_runs(whole(block, o), *(actions if o == peers - 1 else ()))
+
+    def add_near(h, *actions):
+        for p in range(0, peers, 2):
+            add_runs(halves(p, h), *(actions if p == peers - 2 else ()))
 
     first_half, second_half = (0, early), (early, n_group)
     add_peers(order[0], open_up)
-    add_runs(order[3], 0, stay)
-    add_runs(order[0], 0)
+    add_near(early, send_raw)
+    add_runs(whole(order[0], 0))
     add_peers(order[1], lambda: start_pairs(1), meet_far, lambda: relay_some(*first_half, 0))
-    add_runs(order[1], 0, lambda: relay_some(*second_half, 0), lambda: relay_some(*first_half, 1))
-    add_peers(order[2], lambda: start_pairs(2))
-    add_runs(order[2], 0, lambda: relay_some(*second_half, 1))
-    add_peers(order[3], own)
+    add_runs(whole(order[1], 0), lambda: relay_some(*second_half, 0), lambda: relay_some(*first_half, 1))
+    add_near(0, start_third, lambda: relay_some(*second_half, 1))
+    add_runs(whole(block_me, 0), lambda: stay(*first_half))
+    add_peers(block_me, lambda: own(*first_half))
+
+    def act(k):
+        for action in events[k]:
+            action()
 
     index_load.wait()
-    grads_load.wait()
+    sum_runs(0, halves_at, grads_loads)
+    act(0)
 
     def sum_step(q, c):
-        sum_runs(q)
-        for k, actions in events.items():
-
-            @pl.when(q == k)
-            def _():
-                for action in actions:
-                    action()
-
+        sum_runs(q, (pl.ds(0, look),))
+        for k in range(1, len(runs)):
+            if events[k]:
+                pl.when(q == k)(functools.partial(act, k))
         return c
 
-    lax.fori_loop(0, len(runs), sum_step, 0)
-
+    lax.fori_loop(1, len(runs), sum_step, 0)
+
+    add_raw()
+    own(*second_half)
+    stay(*second_half)
     pl.semaphore_wait(far_sem, 1 + inner)
-
-    for_groups(1, pass_second)
-    for_groups(2, pass_third)
+    def late_step(k, c):
+        pl.when(k != inner)(lambda: for_groups(pass_second))
+
+        pl.when(k == inner)(lambda: for_groups(pass_third, 0, early))
+        return c
+
+    lax.fori_loop(0, 2, late_step, 0)
 
     row_wait = pltpu.make_async_remote_copy(
         src_ref=rows_recv.at[pl.ds(0, n_group - 1)], dst_ref=rows_recv.at[pl.ds(0, n_group - 1)],
@@ -320,13 +384,13 @@
 
     row_wait.wait_send()
     tables_load.wait()
-    pair_parts = (BLOCKS - 1) * n_group * (peers - 1)
+    pair_parts = (2 * n_group + early) * (peers - 1)
     pltpu.make_async_remote_copy(
         src_ref=pair.at[pl.ds(0, pair_parts)], dst_ref=pair.at[pl.ds(0, pair_parts)],
         send_sem=pair_send_sem, recv_sem=recv_sem,
         device_id={"group": group, "local": local}, device_id_type=MESH,
     ).wait_send()
-    sent = (BLOCKS - 1) * n_group + buckets - 1
+    sent = 2 * n_group + early + peers * (n_group - early) + buckets - 1
     pltpu.make_async_remote_copy(
         src_ref=sums.at[pl.ds(0, sent)], dst_ref=sums.at[pl.ds(0, sent)],
         send_sem=send_sem, recv_sem=recv_sem,
@@ -339,8 +403,9 @@
             device_id={"group": group, "local": local}, device_id_type=MESH,
         ).wait_recv()
 
-    pl.when(inner == 0)(lambda: wait_parts(n_group * (places - 1) - 1))
-    pl.when(inner == 1)(lambda: wait_parts(n_group * places - 1))
+    for deep in range(2):
+        pl.when((inner == deep) & (group >= early))(lambda: wait_parts(n_group * (places - 2 + deep) - 1))
+        pl.when((inner == deep) & (group < early))(lambda: wait_parts(n_group * (places - 1 + deep) - 1))
     for t in range(2):
         lists = []
         for g in range(n_group):
@@ -368,14 +433,13 @@
         at = pl.ds(i * piece, piece)
         return pltpu.make_async_copy(new.at[t, at], new_tables_hbm.at[t, at], out_sems.at[t, i])
 
-    def step(k, c):
-        t, i = k // PIECES, lax.rem(k, PIECES)
-        at = pl.ds(pl.multiple_of(i * piece, piece), piece)
-        new[t, at] = tables_ref[t, at] - jnp.dot(onehot_ref[t, at], parts_ref[t], preferred_element_type=jnp.float32)
-        out(t, i).start()
-        return c
-
-    lax.fori_loop(0, 2 * PIECES, step, 0)
+    for t in range(2):
+        for i in range(PIECES):
+            at = slice(i * piece, (i + 1) * piece)
+            new[t, at] = tables_ref[t, at] - jnp.dot(
+                onehot_ref[t, at], parts_ref[t], preferred_element_type=jnp.float32
+            )
+            out(t, i).start()
     accums_out.wait()
     for t in range(2):
         for i in range(PIECES):
@@ -411,13 +475,14 @@
             pltpu.VMEM((n_dev, 2, capacity, width), jnp.float32),
             pltpu.VMEM(((BLOCKS - 1) * n_group * (peers - 1), 2, capacity, width), jnp.float32),
             pltpu.VMEM((n_group, 2, capacity, width), jnp.float32),
+            pltpu.VMEM((peers * (n_group - n_group // 2), 2, capacity, width), jnp.float32),
             pltpu.VMEM((n_group * (3 + peers), 2, capacity, width), jnp.float32),
             pltpu.VMEM((n_group, 2, slots), jnp.int32),
             pltpu.VMEM((2, slots, 3 * slots), jnp.bfloat16),
             pltpu.VMEM((2, slots, rows_dev), jnp.float32),
             pltpu.VMEM((2, slots, 128), jnp.float32),
-            dma, dma, dma, dma, dma,
-            dma(((BLOCKS - 1) * n_group,)), dma((n_group,)),
+            dma((2,)), dma, dma, dma, dma,
+            dma(((BLOCKS - 1) * n_group,)), dma((n_group,)), dma,
             dma, dma, dma, dma, dma, regular, regular,
         ],
         compiler_params=pltpu.CompilerParams(

time: 23.6 us -> 22.5 us (0.953)
  Pallas kernels: 22.6 us -> 21.7 us
    pallas_call x1, Pallas kernels: 20.8 us -> 20.1 us  [local_step(): pl.pallas_call(functools.partial(exchange_kernel, n_group, n_local), out_...]
where the time goes in v3:
time: 22.5 us; the launch traced here: 22.3 us
  Pallas kernels  21.7 us (96%)
  between operations  0.64 us (3%)
    pallas_call x1, Pallas kernels, local_step(): pl.pallas_call(functools.partial(exchange_kernel, n_group, n_local), out_...  20.1 us
    pallas_call x1, Pallas kernels, local_step(): pl.pallas_call(update_kernel, out_shape=(jax.ShapeDtypeStruct(tables.shap...  1.61 us

profile of v3, /device:TPU:0, one launch (start us, length us, event | category | flops | bytes accessed | tf_op | source)
XLA Modules:
  0.0 22.3 jit_solution(10883014096922262752)
XLA Ops:
  0.6 20.1 %shard_map.68 = (bf16[2,192,256]{2,1,0:T(8,128)(2,1)S(1)}, bf16[2,1024,192]{2,1,0:T(8,128)(2,1)S(1)}, f32[2,1024,256]{2,1,0:T(8,128)S(1)}, f32[2,1024]{1,0:T(2,128)S(1)}) custom-call(bf16[8192,256]{1,0:T(8,128)(2,1)} %grads_hbm.1, s32[2,8192]{1,0:T(2,128)} %index_hbm.1, s32[2,64]{1,0:T(2,128)} %rows_hbm.1, f32[2,1024,256]{2,1,0:T(8,128)} %tables_hbm.1, ...), custom_call_target="tpu_custom_call" | custom-call | flops 4294967296 | bytes 4194304 | tf_op jit(solution)/shard_map/pallas_call | solution.py:460
  20.7 1.6 %shard_map.69 = (f32[2,1024,256]{2,1,0:T(8,128)}, f32[2,1024]{1,0:T(2,128)}) custom-call(bf16[2,192,256]{2,1,0:T(8,128)(2,1)S(1)} %get-tuple-element.6.parts_ref, bf16[2,1024,192]{2,1,0:T(8,128)(2,1)S(1)} %get-tuple-element.7.onehot_ref, f32[2,1024,256]{2,1,0:T(8,128)S(1)} %get-tuple-element.8.tables_ref, f32[2,1024]{1,0:T(2,128)S(1)} %get-tuple-element.9.accums_ref), custom_call_target="tpu_custom_call" | custom-call | tf_op jit(solution)/shard_map/pallas_call | solution.py:493

commit v4 on v3

--- a/solution.py
+++ b/solution.py
@@ -25,7 +25,7 @@
 def exchange_kernel(
     n_group, n_local, grads_hbm, index_hbm, rows_hbm, tables_hbm, accums_hbm,
     parts_ref, onehot_ref, tables_ref, new_accums_ref,
-    grads, index, rows, accums, sums, pair, relay, raw, recv, rows_recv, same_ref, hit_ref, old_ref,
+    grads, index, rows, accums, sums, pair, relay, raw, recv, rows_recv, acc, same_ref, hit_ref, old_ref,
     grads_sems, index_sem, rows_sem, tables_sem, accums_sem, pair_sems, relay_sems, raw_sem,
     pair_send_sem, send_sem, recv_sem, row_send_sem, row_recv_sem, near_sem, far_sem,
 ):
@@ -77,14 +77,14 @@
     accums_load = pltpu.make_async_copy(accums_hbm, accums, accums_sem)
 
     look = grads.shape[0]
-    halves_at = pl.ds(0, look // 2), pl.ds(look // 2, look - look // 2)
-    grads_loads = [
-        pltpu.make_async_copy(grads_hbm.at[at], grads.at[at], grads_sems.at[k]) for k, at in enumerate(halves_at)
-    ]
+
+    def load(k):
+        at = pl.ds(pl.multiple_of(k * (look // 2), look // 2), look // 2)
+        return pltpu.make_async_copy(grads_hbm.at[at], grads.at[at], grads_sems.at[k])
 
     index_load.start()
-    for grads_load in grads_loads:
-        grads_load.start()
+    for k in range(2):
+        load(k).start()
     rows_load.start()
     accums_load.start()
     barrier = pltpu.get_barrier_semaphore()
@@ -131,27 +131,38 @@
 
     runs, events = [], {}
 
-    def sum_runs(q, cuts, ready=None):
-        first, second = (
+    def part_of(firsts, at):
+        row = lax.broadcasted_iota(jnp.int32, (early * capacity, 1), 0)
+        targets = jnp.concatenate([row + first * capacity for first in firsts], axis=0)
+        onehot = jnp.concatenate(
+            [jnp.where(index[t : t + 1, at] == targets, 1.0, 0.0).astype(jnp.bfloat16) for t in range(2)], axis=0
+        )
+        return jnp.dot(onehot, grads[at, :], preferred_element_type=jnp.float32)
+
+    def keep(firsts, total):
+        n_rows = early * capacity
+        for t in range(2):
+            for i, first in enumerate(firsts):
+                start = (2 * t + i) * n_rows
+                sums[pl.ds(first, early), t] = total[start : start + n_rows, :].reshape(early, capacity, width)
+
+    def sum_runs(q):
+        firsts = tuple(
             functools.reduce(lambda x, k: jnp.where(q == k, runs[k][i], x), range(1, len(runs)), runs[0][i])
             for i in range(2)
         )
-        n_rows = early * capacity
-        row = lax.broadcasted_iota(jnp.int32, (n_rows, 1), 0)
-        targets = jnp.concatenate([row + first * capacity, row + second * capacity], axis=0)
-        total = None
-        for k, at in enumerate(cuts):
-            if ready is not None:
-                ready[k].wait()
-            onehot = jnp.concatenate(
-                [jnp.where(index[t : t + 1, at] == targets, 1.0, 0.0).astype(jnp.bfloat16) for t in range(2)], axis=0
-            )
-            part = jnp.dot(onehot, grads[at, :], preferred_element_type=jnp.float32)
-            total = part if total is None else total + part
-        for t in range(2):
-            for i, at in enumerate((first, second)):
-                start = (2 * t + i) * n_rows
-                sums[pl.ds(at, early), t] = total[start : start + n_rows, :].reshape(early, capacity, width)
+        keep(firsts, part_of(firsts, pl.ds(0, look)))
+
+    def sum_as_loaded(firsts):
+        acc[...] = jnp.zeros_like(acc)
+
+        def one(k, c):
+            load(k).wait()
+            acc[...] += part_of(firsts, pl.ds(pl.multiple_of(k * (look // 2), look // 2), look // 2))
+            return c
+
+        lax.fori_loop(0, 2, one, 0)
+        keep(firsts, acc[...])
 
     def start_pairs(step):
         def one(i, c):
@@ -322,11 +333,11 @@
             action()
 
     index_load.wait()
-    sum_runs(0, halves_at, grads_loads)
+    sum_as_loaded(runs[0])
     act(0)
 
     def sum_step(q, c):
-        sum_runs(q, (pl.ds(0, look),))
+        sum_runs(q)
         for k in range(1, len(runs)):
             if events[k]:
                 pl.when(q == k)(functools.partial(act, k))
@@ -478,6 +489,7 @@
             pltpu.VMEM((peers * (n_group - n_group // 2), 2, capacity, width), jnp.float32),
             pltpu.VMEM((n_group * (3 + peers), 2, capacity, width), jnp.float32),
             pltpu.VMEM((n_group, 2, slots), jnp.int32),
+            pltpu.VMEM((4 * (n_group // 2) * capacity, width), jnp.float32),
             pltpu.VMEM((2, slots, 3 * slots), jnp.bfloat16),
             pltpu.VMEM((2, slots, rows_dev), jnp.float32),
             pltpu.VMEM((2, slots, 128), jnp.float32),

time: 22.5 us -> 22.2 us (0.987)
  Pallas kernels: 21.7 us -> 21.4 us
    pallas_call x1, Pallas kernels: 20.1 us -> 19.8 us  [local_step(): pl.pallas_call(functools.partial(exchange_kernel, n_group, n_local), out_...]
where the time goes in v4:
time: 22.2 us; the launch traced here: 22.1 us
  Pallas kernels  21.4 us (96%)
  between operations  0.64 us (3%)
    pallas_call x1, Pallas kernels, local_step(): pl.pallas_call(functools.partial(exchange_kernel, n_group, n_local), out_...  19.8 us
    pallas_call x1, Pallas kernels, local_step(): pl.pallas_call(update_kernel, out_shape=(jax.ShapeDtypeStruct(tables.shap...  1.61 us

profile of v4, /device:TPU:0, one launch (start us, length us, event | category | flops | bytes accessed | tf_op | source)
XLA Modules:
  0.0 22.1 jit_solution(16276894481838786617)
XLA Ops:
  0.6 19.8 %shard_map.68 = (bf16[2,192,256]{2,1,0:T(8,128)(2,1)S(1)}, bf16[2,1024,192]{2,1,0:T(8,128)(2,1)S(1)}, f32[2,1024,256]{2,1,0:T(8,128)S(1)}, f32[2,1024]{1,0:T(2,128)S(1)}) custom-call(bf16[8192,256]{1,0:T(8,128)(2,1)} %grads_hbm.1, s32[2,8192]{1,0:T(2,128)} %index_hbm.1, s32[2,64]{1,0:T(2,128)} %rows_hbm.1, f32[2,1024,256]{2,1,0:T(8,128)} %tables_hbm.1, ...), custom_call_target="tpu_custom_call" | custom-call | flops 4294967296 | bytes 4194304 | tf_op jit(solution)/shard_map/pallas_call | solution.py:471
  20.5 1.6 %shard_map.69 = (f32[2,1024,256]{2,1,0:T(8,128)}, f32[2,1024]{1,0:T(2,128)}) custom-call(bf16[2,192,256]{2,1,0:T(8,128)(2,1)S(1)} %get-tuple-element.6.parts_ref, bf16[2,1024,192]{2,1,0:T(8,128)(2,1)S(1)} %get-tuple-element.7.onehot_ref, f32[2,1024,256]{2,1,0:T(8,128)S(1)} %get-tuple-element.8.tables_ref, f32[2,1024]{1,0:T(2,128)S(1)} %get-tuple-element.9.accums_ref), custom_call_target="tpu_custom_call" | custom-call | tf_op jit(solution)/shard_map/pallas_call | solution.py:505

commit v5 on v4

--- a/solution.py
+++ b/solution.py
@@ -349,10 +349,12 @@
     own(*second_half)
     stay(*second_half)
     pl.semaphore_wait(far_sem, 1 + inner)
+    second_first = jnp.maximum(inner, 1 - lax.rem(group, 2))
+
     def late_step(k, c):
-        pl.when(k != inner)(lambda: for_groups(pass_second))
-
-        pl.when(k == inner)(lambda: for_groups(pass_third, 0, early))
+        pl.when(k != second_first)(lambda: for_groups(pass_second))
+
+        pl.when(k == second_first)(lambda: for_groups(pass_third, 0, early))
         return c
 
     lax.fori_loop(0, 2, late_step, 0)

time: 22.2 us -> 21.7 us (0.977)
  Pallas kernels: 21.4 us -> 20.8 us
    pallas_call x1, Pallas kernels: 19.8 us -> 19.2 us  [local_step(): pl.pallas_call(functools.partial(exchange_kernel, n_group, n_local), out_...]
where the time goes in v5:
time: 21.7 us; the launch traced here: 21.4 us
  Pallas kernels  20.8 us (96%)
  between operations  0.64 us (3%)
    pallas_call x1, Pallas kernels, local_step(): pl.pallas_call(functools.partial(exchange_kernel, n_group, n_local), out_...  19.2 us
    pallas_call x1, Pallas kernels, local_step(): pl.pallas_call(update_kernel, out_shape=(jax.ShapeDtypeStruct(tables.shap...  1.61 us

profile of v5, /device:TPU:0, one launch (start us, length us, event | category | flops | bytes accessed | tf_op | source)
XLA Modules:
  0.0 21.4 jit_solution(5200034450620837073)
XLA Ops:
  0.6 19.2 %shard_map.68 = (bf16[2,192,256]{2,1,0:T(8,128)(2,1)S(1)}, bf16[2,1024,192]{2,1,0:T(8,128)(2,1)S(1)}, f32[2,1024,256]{2,1,0:T(8,128)S(1)}, f32[2,1024]{1,0:T(2,128)S(1)}) custom-call(bf16[8192,256]{1,0:T(8,128)(2,1)} %grads_hbm.1, s32[2,8192]{1,0:T(2,128)} %index_hbm.1, s32[2,64]{1,0:T(2,128)} %rows_hbm.1, f32[2,1024,256]{2,1,0:T(8,128)} %tables_hbm.1, ...), custom_call_target="tpu_custom_call" | custom-call | flops 4294967296 | bytes 4194304 | tf_op jit(solution)/shard_map/pallas_call | solution.py:473
  19.8 1.6 %shard_map.69 = (f32[2,1024,256]{2,1,0:T(8,128)}, f32[2,1024]{1,0:T(2,128)}) custom-call(bf16[2,192,256]{2,1,0:T(8,128)(2,1)S(1)} %get-tuple-element.6.parts_ref, bf16[2,1024,192]{2,1,0:T(8,128)(2,1)S(1)} %get-tuple-element.7.onehot_ref, f32[2,1024,256]{2,1,0:T(8,128)S(1)} %get-tuple-element.8.tables_ref, f32[2,1024]{1,0:T(2,128)S(1)} %get-tuple-element.9.accums_ref), custom_call_target="tpu_custom_call" | custom-call | tf_op jit(solution)/shard_map/pallas_call | solution.py:507
